TPU v7x, 32 devices: a whole 2x2x4 slice. The times are simulated.
32 devices in a mesh: row: 4 (over z), col: 4 (over x, core), img: 2 (over y).
Axes of the slice: x: 2, y: 2, z: 4, core: 2. Of those that a mesh axis runs over, the one named last changes fastest.
Arguments:
- tokens: bfloat16 [96, 144, 512], P(('img', 'row'), 'col'), parts along dimension 0, may hold values from -6 to 6
- qkv_weight: bfloat16 [2, 512, 1536], P(None, 'col'), may hold values from -0.25 to 0.25
- proj_weight: bfloat16 [2, 512, 512], P(None, 'col'), may hold values from -0.25 to 0.25
- hidden_weight: bfloat16 [2, 512, 2048], P(None, 'col'), may hold values from -0.25 to 0.25
- output_weight: bfloat16 [2, 2048, 512], P(None, 'col'), may hold values from -0.125 to 0.125
- norm_gain: float32 [2, 2, 512], replicated, may hold values from 0.25 to 1.75
- model_bias: float32 [2, 4, 512], replicated, may hold values from -2 to 2
- qkv_bias: float32 [2, 1536], replicated, may hold values from -2 to 2
- hidden_bias: float32 [2, 2048], replicated, may hold values from -2 to 2
- position_bias: float32 [2, 16, 23, 23], replicated, may hold values from -3 to 250
Outputs:
- result: bfloat16 [96, 144, 512], P(('img', 'row'), 'col'), parts along dimension 0
There are 2 independent parts, one for each index of `img`. A program takes and returns all parts, laid end to end along the dimension named above; an argument that names none is the same for every part. Nothing has to cross between parts.
All inputs are finite; a program needn't handle non-finite values.
Results may differ from a plain program's by a relative error of at most 0.012.
Values may be sent and summed in bfloat16 or wider, within the bound.
A program may use at most 192 MiB of HBM per device.

v0:
```python
import functools

import jax
import jax.numpy as jnp
import numpy as np
from jax import lax
from jax.experimental import pallas as pl
from jax.experimental.pallas import tpu as pltpu
from jax.sharding import PartitionSpec as P

HEADS = 16
WIN = 12
SHIFT = 6
HALF = WIN // 2
PATCH = HALF * HALF
AREA = WIN * WIN
GROUP = 4
LOG2E = 1.4426950408889634
MESH = pl.DeviceIdType.MESH


def position_tables(table):
    layers, heads = table.shape[:2]
    coord = np.arange(WIN)
    onehot = (coord[None, :, None] - coord[:, None, None] + WIN - 1 == np.arange(2 * WIN - 1)).astype(np.float32)
    rows = jnp.einsum("kqa,lhab->lhkqb", onehot, table, precision=lax.Precision.HIGHEST)
    both = jnp.einsum("lhkqb,xyb->lhkqxy", rows, onehot, precision=lax.Precision.HIGHEST)
    both = both * LOG2E
    both = both.reshape(layers, heads // GROUP, GROUP, 2, HALF, 2, HALF, 2, HALF, 2, HALF)
    both = both.transpose(0, 1, 3, 7, 4, 8, 2, 5, 9, 6, 10)
    return both.reshape(layers, heads // GROUP, AREA, GROUP * AREA)


def layer_norm(values, gain, shift):
    center = values - jnp.mean(values, -1, keepdims=True)
    spread = jnp.mean(center * center, -1, keepdims=True)
    return center * lax.rsqrt(spread + 1e-05) * gain + shift


def kernel(
    sizes,
    tokens_hbm, qkv_hbm, proj_hbm, hid_hbm, outw_hbm,
    gain_ref, mbias_ref, qkvb_ref, hidb_ref, pos_hbm,
    out_ref,
    wqkv, wproj, whid, wout, pos_ref, tok_ref, tok32, x32, normed, qkv_ref, heads_ref, hidden_ref, y32,
    stage, rowdiff, coldiff,
    sa, sb, sc, ra, rb, rc,
    local_sem, psend, precv, xsend, xrecv, ysend, yrecv, fsend, frecv, hsend, hrecv,
):
    n_row, n_col, n_img = sizes
    chips = n_col // 2
    row, col, img = lax.axis_index("row"), lax.axis_index("col"), lax.axis_index("img")
    chip, core = col // 2, col % 2
    channels = x32.shape[1]
    nwin = x32.shape[0] // AREA
    ncols = 2 * nwin
    partner = {"col": chip * 2 + (1 - core)}
    ypeer = {"img": (img + 1) % n_img}

    def xpeer(t):
        return {"col": lax.rem(chip + t, chips) * 2 + core}

    up, down = lax.rem(row + n_row - 1, n_row), lax.rem(row + 1, n_row)
    left, right = lax.rem(col + n_col - 1, n_col), lax.rem(col + 1, n_col)
    back = ({"row": up}, {"col": left}, {"row": up, "col": left})
    forth = ({"row": down}, {"col": right}, {"row": down, "col": right})

    barrier = pltpu.get_barrier_semaphore()
    greet = [partner, ypeer, *(xpeer(t) for t in range(1, chips)), *back, *forth]
    for target in greet:
        pl.semaphore_signal(barrier, inc=1, device_id=target, device_id_type=MESH)
    tok_copy = pltpu.make_async_copy(tokens_hbm, tok_ref, local_sem.at[8])
    tok_copy.start()
    pl.semaphore_wait(barrier, len(greet))

    hbm = (qkv_hbm, proj_hbm, hid_hbm, outw_hbm)
    vmem = (wqkv, wproj, whid, wout)
    halves = n_img

    def shard(kind, layer, owner):
        rows = hbm[kind].shape[1]
        return vmem[kind].at[layer, pl.ds(pl.multiple_of(owner * rows, rows), rows), :]

    def part(kind, layer, owner, half):
        rows = hbm[kind].shape[1]
        size = rows // halves
        return vmem[kind].at[layer, pl.ds(pl.multiple_of(owner * rows + half * size, size), size), :]

    def remote(src, dst, send, recv, target):
        return pltpu.make_async_remote_copy(
            src_ref=src, dst_ref=dst, send_sem=send, recv_sem=recv, device_id=target, device_id_type=MESH
        )

    sends = []
    for t in range(8):
        layer, kind = divmod(t, 4)
        rows = hbm[kind].shape[1]
        size = rows // halves
        mine = hbm[kind].at[layer, pl.ds(pl.multiple_of(img * size, size), size), :]
        for d in range(1, chips):
            copy = remote(mine, part(kind, layer, col, img), xsend.at[t, d - 1], xrecv.at[t, d - 1], xpeer(d))
            copy.start()
            sends.append(copy)
        copy = remote(hbm[kind].at[layer], shard(kind, layer, col), psend.at[t], precv.at[t], partner)
        copy.start()
        sends.append(copy)
        pltpu.make_async_copy(hbm[kind].at[layer], shard(kind, layer, col), local_sem.at[t]).start()
        if t == 0:
            pos_copy = pltpu.make_async_copy(pos_hbm, pos_ref, local_sem.at[9])
            pos_copy.start()

    def owner_at(d, lane):
        return lax.rem(chip + chips - d, chips) * 2 + lane

    def forward_x(t):
        layer, kind = divmod(t, 4)
        for d in range(1, chips):
            got = part(kind, layer, owner_at(d, core), img)
            remote(got, got, xsend.at[t, d - 1], xrecv.at[t, d - 1], xpeer(d)).wait_recv()
            for copy in (
                remote(got, got, ysend.at[t, d - 1], yrecv.at[t, d - 1], ypeer),
                remote(got, got, fsend.at[t, d - 1, 0], frecv.at[t, d - 1, 0], partner),
            ):
                copy.start()
                sends.append(copy)

    def forward_y(t):
        layer, kind = divmod(t, 4)
        for d in range(1, chips):
            got = part(kind, layer, owner_at(d, core), 1 - img)
            remote(got, got, ysend.at[t, d - 1], yrecv.at[t, d - 1], ypeer).wait_recv()
            copy = remote(got, got, fsend.at[t, d - 1, 1], frecv.at[t, d - 1, 1], partner)
            copy.start()
            sends.append(copy)

    def ready(t):
        layer, kind = divmod(t, 4)
        pltpu.make_async_copy(hbm[kind].at[layer], shard(kind, layer, col), local_sem.at[t]).wait()
        other = shard(kind, layer, chip * 2 + (1 - core))
        remote(other, other, psend.at[t], precv.at[t], partner).wait_recv()
        for d in range(1, chips):
            for k, half in ((0, img), (1, 1 - img)):
                got = part(kind, layer, owner_at(d, 1 - core), half)
                remote(got, got, fsend.at[t, d - 1, k], frecv.at[t, d - 1, k], partner).wait_recv()

    def iota(shape, dim):
        return lax.broadcasted_iota(jnp.int32, shape, dim)

    wide = GROUP * AREA
    key = iota((AREA, wide), 0)
    query = iota((AREA, wide), 1) % AREA
    rowdiff[...] = ((key // (2 * PATCH)) != (query // (2 * PATCH))).astype(jnp.float32)
    coldiff[...] = (((key // PATCH) % 2) != ((query // PATCH) % 2)).astype(jnp.float32)
    pick = (key == query).astype(jnp.bfloat16)
    head_dim = channels // HEADS
    lanes = GROUP * head_dim
    own_head = iota((lanes, wide), 0) // head_dim == iota((lanes, wide), 1) // AREA
    head_masks = [(iota((AREA, lanes), 1) // head_dim == h).astype(jnp.bfloat16) for h in range(GROUP)]
    last_row = (row == n_row - 1).astype(jnp.float32)
    last_col = (col == n_col - 1).astype(jnp.float32)

    def base(half, patch_col):
        return (patch_col // 2) * AREA + half * 2 * PATCH + (patch_col % 2) * PATCH

    tok_copy.wait()
    tok32[...] = tok_ref[...].astype(jnp.float32)
    for r in range(WIN):
        for p in range(ncols):
            start = base(r // HALF, p) + (r % HALF) * HALF
            x32[start : start + HALF, :] = tok32[r, p * HALF : (p + 1) * HALF, :]

    def block(layer, hooks):
        for w in range(nwin):
            rows = slice(w * AREA, (w + 1) * AREA)
            normed[rows, :] = layer_norm(
                x32[rows, :], gain_ref[layer, 0:1, :], mbias_ref[layer, 0:1, :]
            ).astype(jnp.bfloat16)
        hooks[0]()
        for c in range(3):
            cols = slice(c * channels, (c + 1) * channels)
            qkv_ref[:, cols] = (
                jnp.dot(normed[...], wqkv[layer, :, cols], preferred_element_type=jnp.float32)
                + qkvb_ref[layer : layer + 1, cols]
            ).astype(jnp.bfloat16)
        if layer == 0:
            pos_copy.wait()
        for w in range(nwin):
            hooks[1 + w]()
            rows = slice(w * AREA, (w + 1) * AREA)

            def one_group(g, carry):
                def lanes_of(which):
                    first = pl.multiple_of(which * channels + g * lanes, lanes)
                    return qkv_ref[rows, pl.ds(first, lanes)]

                q, k, v = lanes_of(0), lanes_of(1), lanes_of(2)
                stacked = jnp.concatenate([q * m for m in head_masks], axis=0)
                scores = lax.dot_general(
                    k, stacked, (((1,), (1,)), ((), ())), preferred_element_type=jnp.float32
                )
                scores = scores * (LOG2E / float(np.sqrt(head_dim))) + pos_ref[layer, g]
                if layer == 1:
                    differs = rowdiff[...] * last_row
                    if w == nwin - 1:
                        differs = differs + coldiff[...] * last_col
                    scores = jnp.where(differs > 0.0, -1000000000.0 * LOG2E, scores)
                top = jnp.max(scores, axis=0, keepdims=True)
                weight = jnp.exp2(scores - top)
                total = jnp.sum(weight, axis=0, keepdims=True)
                mixed = lax.dot_general(
                    v, weight.astype(jnp.bfloat16), (((0,), (0,)), ((), ())), preferred_element_type=jnp.float32
                )
                mixed = jnp.where(own_head, mixed * (1.0 / total), 0.0).astype(jnp.bfloat16)
                gathered = lax.dot_general(
                    pick, mixed, (((1,), (1,)), ((), ())), preferred_element_type=jnp.float32
                )
                heads_ref[rows, pl.ds(pl.multiple_of(g * lanes, lanes), lanes)] = gathered.astype(jnp.bfloat16)
                return carry

            lax.fori_loop(0, HEADS // GROUP, one_group, 0)
        hooks[1 + nwin]()
        y32[...] = x32[...] + (
            jnp.dot(heads_ref[...], wproj[layer], preferred_element_type=jnp.float32)
            + mbias_ref[layer, 2:3, :]
        )
        for w in range(nwin):
            rows = slice(w * AREA, (w + 1) * AREA)
            normed[rows, :] = layer_norm(
                y32[rows, :], gain_ref[layer, 1:2, :], mbias_ref[layer, 1:2, :]
            ).astype(jnp.bfloat16)
        hooks[2 + nwin]()
        chunk = 512
        for c in range(whid.shape[2] // chunk):
            cols = slice(c * chunk, (c + 1) * chunk)
            pre = (
                jnp.dot(normed[...], whid[layer, :, cols], preferred_element_type=jnp.float32)
                + hidb_ref[layer : layer + 1, cols]
            )
            hidden_ref[:, cols] = (0.5 * pre * (1.0 + lax.erf(pre * float(np.sqrt(0.5))))).astype(jnp.bfloat16)
        hooks[3 + nwin]()
        final = y32[...] + (
            jnp.dot(hidden_ref[...], wout[layer], preferred_element_type=jnp.float32)
            + mbias_ref[layer, 3:4, :]
        )
        y32[...] = final.astype(jnp.bfloat16).astype(jnp.float32)

    def exchange(k, targets, patches):
        copies = []
        bufs = ((sa, ra), (sb, rb), (sc, rc))
        for which, (source, landing) in enumerate(bufs):
            listed = patches[which]
            for at, (half, p) in enumerate(listed):
                first = base(half, p)
                stage[at * PATCH : (at + 1) * PATCH, :] = y32[first : first + PATCH, :]
            source[k] = stage[0 : len(listed) * PATCH, :].astype(jnp.bfloat16)
            copy = remote(source.at[k], landing.at[k], hsend.at[k, which], hrecv.at[k, which], targets[which])
            copy.start()
            copies.append(copy)
        return copies

    def nothing():
        pass

    def steps(*calls):
        def run():
            for call, t in calls:
                call(t)

        return run

    block(0, [
        steps((forward_x, 0), (forward_x, 1), (forward_y, 0), (ready, 0)),
        steps((forward_y, 1)),
        steps((forward_x, 2)),
        nothing,
        steps((forward_x, 3), (forward_y, 2), (ready, 1)),
        steps((ready, 2),),
        steps((forward_y, 3), (forward_x, 4), (ready, 3)),
    ])
    copies = exchange(0, back, (
        [(0, p) for p in range(1, ncols)], [(1, 0)], [(0, 0)],
    ))
    for p in range(1, ncols):
        first, at = base(1, p), base(0, p - 1)
        x32[at : at + PATCH, :] = y32[first : first + PATCH, :]
    steps((forward_y, 4), (forward_x, 5), (forward_x, 6), (forward_y, 5))()
    for copy in copies:
        copy.wait()
    stage[...] = ra[0].astype(jnp.float32)
    for p in range(ncols - 1):
        at = base(1, p)
        x32[at : at + PATCH, :] = stage[p * PATCH : (p + 1) * PATCH, :]
    at = base(0, ncols - 1)
    x32[at : at + PATCH, :] = rb[0].astype(jnp.float32)
    at = base(1, ncols - 1)
    x32[at : at + PATCH, :] = rc[0].astype(jnp.float32)

    block(1, [
        steps((ready, 4)),
        steps((forward_y, 6)),
        steps((forward_x, 7)),
        nothing,
        steps((forward_y, 7), (ready, 5)),
        steps((ready, 6),),
        steps((ready, 7)),
    ])
    copies = exchange(1, forth, (
        [(1, p) for p in range(ncols - 1)], [(0, ncols - 1)], [(1, ncols - 1)],
    ))

    def put(source, start, half, p):
        for r in range(HALF):
            tok32[half * HALF + r, p * HALF : (p + 1) * HALF, :] = source[
                start + r * HALF : start + (r + 1) * HALF, :
            ]

    for p in range(ncols - 1):
        put(y32, base(0, p), 1, p + 1)
    for copy in copies:
        copy.wait()
    stage[...] = ra[1].astype(jnp.float32)
    for p in range(ncols - 1):
        put(stage, p * PATCH, 0, p + 1)
    stage[0:PATCH, :] = rb[1].astype(jnp.float32)
    stage[PATCH : 2 * PATCH, :] = rc[1].astype(jnp.float32)
    put(stage, 0, 1, 0)
    put(stage, PATCH, 0, 0)
    out_ref[...] = tok32[...].astype(jnp.bfloat16)
    for copy in sends:
        copy.wait_send()


def local(sizes, tokens, qkv_w, proj_w, hid_w, out_w, gain, mbias, qkvb, hidb, position):
    pos = position_tables(position)
    n_col, n_img = sizes[1], sizes[2]
    chips = n_col // 2
    height, width, channels = tokens.shape
    count = height * width
    f32, bf16 = jnp.float32, jnp.bfloat16
    hop = (width // HALF - 1) * PATCH
    dma = pltpu.SemaphoreType.DMA

    def full(w):
        return pltpu.VMEM((w.shape[0], w.shape[1] * n_col, w.shape[2]), bf16)

    any_spec = pl.BlockSpec(memory_space=pl.ANY)
    vmem_spec = pl.BlockSpec(memory_space=pltpu.VMEM)
    return pl.pallas_call(
        functools.partial(kernel, sizes),
        out_shape=jax.ShapeDtypeStruct(tokens.shape, bf16),
        in_specs=[any_spec] * 5 + [vmem_spec] * 4 + [any_spec],
        out_specs=vmem_spec,
        scratch_shapes=[
            full(qkv_w), full(proj_w), full(hid_w), full(out_w),
            pltpu.VMEM(pos.shape, f32),
            pltpu.VMEM(tokens.shape, bf16),
            pltpu.VMEM(tokens.shape, f32),
            pltpu.VMEM((count, channels), f32),
            pltpu.VMEM((count, channels), bf16),
            pltpu.VMEM((count, 3 * channels), bf16),
            pltpu.VMEM((count, channels), bf16),
            pltpu.VMEM((count, hid_w.shape[2]), bf16),
            pltpu.VMEM((count, channels), f32),
            pltpu.VMEM((hop, channels), f32),
            pltpu.VMEM((AREA, GROUP * AREA), f32),
            pltpu.VMEM((AREA, GROUP * AREA), f32),
            pltpu.VMEM((2, hop, channels), bf16),
            pltpu.VMEM((2, PATCH, channels), bf16),
            pltpu.VMEM((2, PATCH, channels), bf16),
            pltpu.VMEM((2, hop, channels), bf16),
            pltpu.VMEM((2, PATCH, channels), bf16),
            pltpu.VMEM((2, PATCH, channels), bf16),
            dma((10,)),
            dma((8,)), dma((8,)),
            dma((8, chips - 1)), dma((8, chips - 1)),
            dma((8, chips - 1)), dma((8, chips - 1)),
            dma((8, chips - 1, 2)), dma((8, chips - 1, 2)),
            dma((2, 3)), dma((2, 3)),
        ],
        compiler_params=pltpu.CompilerParams(
            collective_id=0, has_side_effects=True, vmem_limit_bytes=62 * 1024 * 1024
        ),
        name="swin_pair",
    )(tokens, qkv_w, proj_w, hid_w, out_w, gain, mbias, qkvb, hidb, pos)


def solution(mesh):
    in_specs = (P(("img", "row"), "col", None),) + (P(None, "col", None),) * 4 + (P(),) * 5
    sizes = tuple(mesh.shape[a] for a in ("row", "col", "img"))
    return jax.shard_map(
        functools.partial(local, sizes),
        mesh=mesh,
        in_specs=in_specs,
        out_specs=P(("img", "row"), "col", None),
        check_vma=False,
    )
```

profile of v0, /device:TPU:0, one launch (start us, length us, event | category | flops | bytes accessed | tf_op | source)
XLA Modules:
  0.0 263.8 jit_solution(4053953429528597552)
XLA Ops:
  0.0 0.0 copy-start
  0.0 0.0 copy-start.2
  0.0 1.0 copy-done
  1.0 3.5 %fusion.2 = f32[12,12,2,16,23]{4,1,3,2,0:T(8,128)S(1)} fusion(f32[12,12,23,1,1]{2,1,4,3,0:T(8,128)} %constant.6, f32[2,16,23,23,1]{3,1,2,0,4:T(8,128)S(1)} %bitcast.21), kind=kOutput, calls=%fused_computation.3 | convolution fusion | flops 29251584 | bytes 504896 | tf_op jit(solution)/shard_map/kqa,lhab->lhkqb/dot_general | solution.py:26
  4.5 0.0 copy-done.2
  4.5 26.5 %convolution_multiply_fusion = f32[2,16,12,12,12,12]{5,1,4,3,2,0:T(8,128)} fusion(f32[12,12,23,1,1,1]{2,1,0,5,4,3:T(8,128)S(1)} %copy-done.2, f32[12,12,2,16,23]{4,1,3,2,0:T(8,128)S(1)} %fusion.2), kind=kOutput, calls=%fused_computation | convolution fusion | flops 183803904 | bytes 3091392 | tf_op jit(solution)/shard_map/lhkqb,xyb->lhkqxy/dot_general | solution.py:27
  31.0 53.3 %reshape.6 = f32[2,4,4,2,6,2,6,2,6,2,6]{10,9,2,1,8,7,6,5,4,3,0:T(2,128)} reshape(f32[2,16,12,12,12,12]{5,1,4,3,2,0:T(8,128)} %convolution_multiply_fusion) | data formatting | bytes 5308416 | tf_op jit(solution)/shard_map/reshape | solution.py:29
  84.3 60.7 %copy.14 = f32[2,4,2,2,6,6,4,2,2,6,6]{10,9,8,7,6,5,4,3,2,1,0:T(8,128)} copy(f32[2,4,2,2,6,6,4,2,2,6,6]{10,8,6,1,5,3,9,7,4,2,0:T(2,128)} %bitcast.22) | data formatting | bytes 5308416 | tf_op jit(solution)/shard_map/transpose | solution.py:30
  144.9 0.0 copy-start.1
  145.0 45.0 %reshape.7.pos_hbm = f32[2,4,144,576]{3,2,1,0:T(8,128)} reshape(f32[2,4,2,2,6,6,4,2,2,6,6]{10,9,8,7,6,5,4,3,2,1,0:T(8,128)} %copy.14) | data formatting | bytes 5308416 | tf_op jit(solution)/shard_map/reshape | solution.py:31
  190.0 71.9 %swin_pair.1 = bf16[12,36,512]{2,1,0:T(8,128)(2,1)} custom-call(bf16[12,36,512]{2,1,0:T(8,128)(2,1)} %tokens_hbm.1, bf16[2,128,1536]{2,1,0:T(8,128)(2,1)} %qkv_hbm.1, bf16[2,128,512]{2,1,0:T(8,128)(2,1)} %proj_hbm.1, bf16[2,128,2048]{2,1,0:T(8,128)(2,1)} %hid_hbm.1, bf16[2,512,512]{2,1,0:T(8,128)(2,1)} %outw_hbm.1, f32[2,2,512]{2,1,0:T(2,128)} %gain_ref.1, ...), custom_call_target="tpu_custom_call" | custom-call | tf_op jit(solution)/shard_map/swin_pair/pallas_call | solution.py:348
  261.9 1.8 copy.27
  263.8 0.0 copy-done.1
Async XLA Ops:
  0.0 1.0 copy-start
  0.0 4.5 %copy-start.2 = (f32[12,12,23,1,1,1]{2,1,0,5,4,3:T(8,128)S(1)}, f32[12,12,23,1,1,1]{2,1,0,5,4,3:T(8,128)}, u32[]{:S(2)}) copy-start(f32[12,12,23,1,1,1]{2,1,0,5,4,3:T(8,128)} %constant.7) | copy-start | bytes 39748
  144.9 118.8 %copy-start.1 = (f32[2,16,23,23]{3,1,2,0:T(8,128)S(1)}, f32[2,16,23,23]{3,1,2,0:T(8,128)}, u32[]{:S(2)}) copy-start(f32[2,16,23,23]{3,1,2,0:T(8,128)} %param.21) | copy-start | bytes 203140
where the time goes:
time: 266 us; the launch traced here: 264 us
  local copies, waits for them, and re-layouts  162 us (61%)
  Pallas kernels  71.9 us (27%)
  matrix products  30 us (11%)
    pallas_call x1, Pallas kernels, local(): pl.pallas_call(functools.partial(kernel, sizes), out_shape=jax.ShapeDtype...  71.9 us
    transpose x1, local copies, waits for them, and re-layouts, position_tables(): both = both.transpose(0, 1, 3, 7, 4, 8, 2, 5, 9, 6, 10)  60.7 us
    reshape x1, local copies, waits for them, and re-layouts, position_tables(): both.reshape(layers, heads // GROUP, GROUP, 2, HALF, 2, HALF, 2, HALF, 2,...  53.3 us
    reshape x1, local copies, waits for them, and re-layouts, position_tables(): return both.reshape(layers, heads // GROUP, AREA, GROUP * AREA)  45 us
    dot_general x1, matrix products, position_tables(): jnp.einsum('lhkqb,xyb->lhkqxy', rows, onehot, precision=lax.Precision.HIG...  26.5 us

commit v1 on v0

--- a/solution.py
+++ b/solution.py
@@ -19,16 +19,13 @@
 MESH = pl.DeviceIdType.MESH
 
 
-def position_tables(table):
-    layers, heads = table.shape[:2]
-    coord = np.arange(WIN)
-    onehot = (coord[None, :, None] - coord[:, None, None] + WIN - 1 == np.arange(2 * WIN - 1)).astype(np.float32)
-    rows = jnp.einsum("kqa,lhab->lhkqb", onehot, table, precision=lax.Precision.HIGHEST)
-    both = jnp.einsum("lhkqb,xyb->lhkqxy", rows, onehot, precision=lax.Precision.HIGHEST)
-    both = both * LOG2E
-    both = both.reshape(layers, heads // GROUP, GROUP, 2, HALF, 2, HALF, 2, HALF, 2, HALF)
-    both = both.transpose(0, 1, 3, 7, 4, 8, 2, 5, 9, 6, 10)
-    return both.reshape(layers, heads // GROUP, AREA, GROUP * AREA)
+def position_rows(table):
+    layers, heads, span, _ = table.shape
+    groups = heads // GROUP
+    flipped = (table * LOG2E)[:, :, :, ::-1].reshape(layers, groups, GROUP, span, span)
+    flipped = jnp.pad(flipped.transpose(0, 1, 4, 2, 3), ((0, 0), (0, 0), (0, 1), (0, 0), (0, 1)))
+    flat = flipped.reshape(layers * groups * 2 * WIN, GROUP * 2 * WIN)
+    return jnp.pad(flat, ((0, 0), (0, 128 - flat.shape[1])))
 
 
 def layer_norm(values, gain, shift):
@@ -40,10 +37,10 @@
 def kernel(
     sizes,
     tokens_hbm, qkv_hbm, proj_hbm, hid_hbm, outw_hbm,
-    gain_ref, mbias_ref, qkvb_ref, hidb_ref, pos_hbm,
+    gain_ref, mbias_ref, qkvb_ref, hidb_ref, table_ref,
     out_ref,
     wqkv, wproj, whid, wout, pos_ref, tok_ref, tok32, x32, normed, qkv_ref, heads_ref, hidden_ref, y32,
-    stage, rowdiff, coldiff,
+    stage, rowdiff, coldiff, zrows,
     sa, sb, sc, ra, rb, rc,
     local_sem, psend, precv, xsend, xrecv, ysend, yrecv, fsend, frecv, hsend, hrecv,
 ):
@@ -105,9 +102,6 @@
         copy.start()
         sends.append(copy)
         pltpu.make_async_copy(hbm[kind].at[layer], shard(kind, layer, col), local_sem.at[t]).start()
-        if t == 0:
-            pos_copy = pltpu.make_async_copy(pos_hbm, pos_ref, local_sem.at[9])
-            pos_copy.start()
 
     def owner_at(d, lane):
         return lax.rem(chip + chips - d, chips) * 2 + lane
@@ -168,6 +162,42 @@
         for p in range(ncols):
             start = base(r // HALF, p) + (r % HALF) * HALF
             x32[start : start + HALF, :] = tok32[r, p * HALF : (p + 1) * HALF, :]
+
+    span = 2 * WIN
+    high = table_ref[...].astype(jnp.bfloat16)
+    rest = table_ref[...] - high.astype(jnp.float32)
+    middle = rest.astype(jnp.bfloat16)
+    low = (rest - middle.astype(jnp.float32)).astype(jnp.bfloat16)
+    thirds = jnp.concatenate([high, middle, low], axis=0)
+    count = table_ref.shape[0]
+
+    def positions(rb):
+        slot = iota((table_ref.shape[1], wide), 0)
+        lane = iota((table_ref.shape[1], wide), 1)
+        at = lane % AREA
+        ra = (at // (2 * PATCH)) * HALF + (at % PATCH) // HALF
+        onehot = (slot == (lane // AREA) * span + ra - rb + WIN - 1).astype(jnp.bfloat16)
+        found = jnp.dot(thirds, onehot, preferred_element_type=jnp.float32)
+        found = found[:count] + found[count : 2 * count] + found[2 * count :]
+        zrows[...] = found.reshape(zrows.shape)
+        inner = iota((1, wide), 1) % AREA
+        ca = ((inner // PATCH) % 2) * HALF + inner % HALF
+
+        def one(n, carry):
+            rows = jnp.zeros((WIN, wide), jnp.float32)
+            for v in range(WIN):
+                rows = jnp.where(ca == v, zrows[n, WIN - 1 - v : 2 * WIN - 1 - v, :], rows)
+            groups = HEADS // GROUP
+            for pc in range(2):
+                first = (rb // HALF) * 2 * PATCH + pc * PATCH + (rb % HALF) * HALF
+                pos_ref[n // groups, n % groups, first : first + HALF, :] = rows[pc * HALF : (pc + 1) * HALF]
+            return carry
+
+        lax.fori_loop(0, zrows.shape[0], one, 0)
+
+    def position_range(rows):
+        for rb in rows:
+            positions(rb)
 
     def block(layer, hooks):
         for w in range(nwin):
@@ -182,8 +212,6 @@
                 jnp.dot(normed[...], wqkv[layer, :, cols], preferred_element_type=jnp.float32)
                 + qkvb_ref[layer : layer + 1, cols]
             ).astype(jnp.bfloat16)
-        if layer == 0:
-            pos_copy.wait()
         for w in range(nwin):
             hooks[1 + w]()
             rows = slice(w * AREA, (w + 1) * AREA)
@@ -269,7 +297,10 @@
         return run
 
     block(0, [
-        steps((forward_x, 0), (forward_x, 1), (forward_y, 0), (ready, 0)),
+        steps(
+            (position_range, range(0, 5)), (forward_x, 0), (position_range, range(5, 8)), (forward_x, 1),
+            (position_range, range(8, WIN)), (forward_y, 0), (ready, 0),
+        ),
         steps((forward_y, 1)),
         steps((forward_x, 2)),
         nothing,
@@ -331,7 +362,7 @@
 
 
 def local(sizes, tokens, qkv_w, proj_w, hid_w, out_w, gain, mbias, qkvb, hidb, position):
-    pos = position_tables(position)
+    table = position_rows(position)
     n_col, n_img = sizes[1], sizes[2]
     chips = n_col // 2
     height, width, channels = tokens.shape
@@ -348,11 +379,11 @@
     return pl.pallas_call(
         functools.partial(kernel, sizes),
         out_shape=jax.ShapeDtypeStruct(tokens.shape, bf16),
-        in_specs=[any_spec] * 5 + [vmem_spec] * 4 + [any_spec],
+        in_specs=[any_spec] * 5 + [vmem_spec] * 5,
         out_specs=vmem_spec,
         scratch_shapes=[
             full(qkv_w), full(proj_w), full(hid_w), full(out_w),
-            pltpu.VMEM(pos.shape, f32),
+            pltpu.VMEM((2, HEADS // GROUP, AREA, GROUP * AREA), f32),
             pltpu.VMEM(tokens.shape, bf16),
             pltpu.VMEM(tokens.shape, f32),
             pltpu.VMEM((count, channels), f32),
@@ -364,6 +395,7 @@
             pltpu.VMEM((hop, channels), f32),
             pltpu.VMEM((AREA, GROUP * AREA), f32),
             pltpu.VMEM((AREA, GROUP * AREA), f32),
+            pltpu.VMEM((2 * HEADS // GROUP, 2 * WIN, GROUP * AREA), f32),
             pltpu.VMEM((2, hop, channels), bf16),
             pltpu.VMEM((2, PATCH, channels), bf16),
             pltpu.VMEM((2, PATCH, channels), bf16),
@@ -381,7 +413,7 @@
             collective_id=0, has_side_effects=True, vmem_limit_bytes=62 * 1024 * 1024
         ),
         name="swin_pair",
-    )(tokens, qkv_w, proj_w, hid_w, out_w, gain, mbias, qkvb, hidb, pos)
+    )(tokens, qkv_w, proj_w, hid_w, out_w, gain, mbias, qkvb, hidb, table)
 
 
 def solution(mesh):

time: 266 us -> 77.3 us (0.29)
  local copies, waits for them, and re-layouts: 162 us -> 4.25 us
  matrix products: 30 us -> 0 us
    reshape x2, local copies, waits for them, and re-layouts: 98.3 us -> 0.53 us  [the longest x1 0.33 us: position_rows(): (table * LOG2E)[:, :, :, ::-1].reshape(layers, groups, GROUP, span, span)]
    transpose x1 -> x0, local copies, waits for them, and re-layouts: 60.7 us -> none  [position_tables(): both = both.transpose(0, 1, 3, 7, 4, 8, 2, 5, 9, 6, 10)]
    dot_general x2 -> x0, matrix products: 30 us -> none  [the longest x1 26.5 us: position_tables(): jnp.einsum('lhkqb,xyb->lhkqxy', rows, onehot, precision=lax.Precision.HIG...]
where the time goes in v1:
time: 77.3 us; the launch traced here: 77.1 us
  Pallas kernels  72.8 us (94%)
  local copies, waits for them, and re-layouts  4.25 us (5%)
    pallas_call x1, Pallas kernels, local(): pl.pallas_call(functools.partial(kernel, sizes), out_shape=jax.ShapeDtype...  72.8 us
    unnamed x1, local copies, waits for them, and re-layouts  1.84 us

profile of v1, /device:TPU:0, one launch (start us, length us, event | category | flops | bytes accessed | tf_op | source)
XLA Modules:
  0.0 77.1 jit_solution(15360035946012061226)
XLA Ops:
  0.0 1.1 %reverse.3 = f32[2,16,23,23]{3,1,2,0:T(8,128)S(1)} reverse(f32[2,16,23,23]{3,1,2,0:T(8,128)} %param.19), dimensions={3} | reverse | bytes 135424 | tf_op jit(solution)/shard_map/reverse
  1.2 0.3 copy.11
  1.5 0.1 pad.8
  1.6 0.2 reshape.7
  1.8 0.7 pad.9.table_ref
  2.5 72.8 %swin_pair.1 = bf16[12,36,512]{2,1,0:T(8,128)(2,1)} custom-call(bf16[12,36,512]{2,1,0:T(8,128)(2,1)} %tokens_hbm.1, bf16[2,128,1536]{2,1,0:T(8,128)(2,1)} %qkv_hbm.1, bf16[2,128,512]{2,1,0:T(8,128)(2,1)} %proj_hbm.1, bf16[2,128,2048]{2,1,0:T(8,128)(2,1)} %hid_hbm.1, bf16[2,512,512]{2,1,0:T(8,128)(2,1)} %outw_hbm.1, f32[2,2,512]{2,1,0:T(2,128)} %gain_ref.1, ...), custom_call_target="tpu_custom_call" | custom-call | tf_op jit(solution)/shard_map/swin_pair/pallas_call | solution.py:379
  75.3 1.8 %copy.13 = bf16[12,36,512]{2,1,0:T(8,128)(2,1)} copy(bf16[12,36,512]{2,1,0:T(8,128)(2,1)} %swin_pair.1) | data formatting | bytes 884736
  (1 shorter events, 0.0 us)

commit v2 on v1

--- a/solution.py
+++ b/solution.py
@@ -245,7 +245,7 @@
                 heads_ref[rows, pl.ds(pl.multiple_of(g * lanes, lanes), lanes)] = gathered.astype(jnp.bfloat16)
                 return carry
 
-            lax.fori_loop(0, HEADS // GROUP, one_group, 0)
+            lax.fori_loop(0, HEADS // GROUP, one_group, 0, unroll=4)
         hooks[1 + nwin]()
         y32[...] = x32[...] + (
             jnp.dot(heads_ref[...], wproj[layer], preferred_element_type=jnp.float32)
@@ -299,14 +299,14 @@
     block(0, [
         steps(
             (position_range, range(0, 5)), (forward_x, 0), (position_range, range(5, 8)), (forward_x, 1),
-            (position_range, range(8, WIN)), (forward_y, 0), (ready, 0),
+            (position_range, range(8, WIN)), (forward_y, 0), (forward_x, 2), (ready, 0),
         ),
         steps((forward_y, 1)),
-        steps((forward_x, 2)),
         nothing,
-        steps((forward_x, 3), (forward_y, 2), (ready, 1)),
-        steps((ready, 2),),
-        steps((forward_y, 3), (forward_x, 4), (ready, 3)),
+        steps((forward_x, 3), (forward_y, 2)),
+        steps((ready, 1)),
+        steps((forward_x, 4), (ready, 2)),
+        steps((forward_y, 3), (forward_x, 5), (ready, 3)),
     ])
     copies = exchange(0, back, (
         [(0, p) for p in range(1, ncols)], [(1, 0)], [(0, 0)],
@@ -314,7 +314,7 @@
     for p in range(1, ncols):
         first, at = base(1, p), base(0, p - 1)
         x32[at : at + PATCH, :] = y32[first : first + PATCH, :]
-    steps((forward_y, 4), (forward_x, 5), (forward_x, 6), (forward_y, 5))()
+    steps((forward_y, 4), (forward_x, 6), (forward_y, 5))()
     for copy in copies:
         copy.wait()
     stage[...] = ra[0].astype(jnp.float32)
@@ -327,12 +327,12 @@
     x32[at : at + PATCH, :] = rc[0].astype(jnp.float32)
 
     block(1, [
-        steps((ready, 4)),
+        steps((ready, 4), (forward_x, 7)),
         steps((forward_y, 6)),
-        steps((forward_x, 7)),
         nothing,
-        steps((forward_y, 7), (ready, 5)),
-        steps((ready, 6),),
+        steps((forward_y, 7)),
+        steps((ready, 5)),
+        steps((ready, 6)),
         steps((ready, 7)),
     ])
     copies = exchange(1, forth, (

time: 77.3 us -> 68.4 us (0.88)
  Pallas kernels: 72.8 us -> 63.9 us
    pallas_call x1, Pallas kernels: 72.8 us -> 63.9 us  [local(): pl.pallas_call(functools.partial(kernel, sizes), out_shape=jax.ShapeDtype...]
where the time goes in v2:
time: 68.4 us; the launch traced here: 68.2 us
  Pallas kernels  63.9 us (93%)
  local copies, waits for them, and re-layouts  4.25 us (6%)
    pallas_call x1, Pallas kernels, local(): pl.pallas_call(functools.partial(kernel, sizes), out_shape=jax.ShapeDtype...  63.9 us
    unnamed x1, local copies, waits for them, and re-layouts  1.84 us

profile of v2, /device:TPU:0, one launch (start us, length us, event | category | flops | bytes accessed | tf_op | source)
XLA Modules:
  0.0 68.2 jit_solution(16011150758828639127)
XLA Ops:
  0.0 1.1 %reverse.3 = f32[2,16,23,23]{3,1,2,0:T(8,128)S(1)} reverse(f32[2,16,23,23]{3,1,2,0:T(8,128)} %param.19), dimensions={3} | reverse | bytes 135424 | tf_op jit(solution)/shard_map/reverse
  1.2 0.3 copy.11
  1.5 0.1 pad.8
  1.6 0.2 reshape.7
  1.8 0.7 pad.9.table_ref
  2.5 63.9 %swin_pair.1 = bf16[12,36,512]{2,1,0:T(8,128)(2,1)} custom-call(bf16[12,36,512]{2,1,0:T(8,128)(2,1)} %tokens_hbm.1, bf16[2,128,1536]{2,1,0:T(8,128)(2,1)} %qkv_hbm.1, bf16[2,128,512]{2,1,0:T(8,128)(2,1)} %proj_hbm.1, bf16[2,128,2048]{2,1,0:T(8,128)(2,1)} %hid_hbm.1, bf16[2,512,512]{2,1,0:T(8,128)(2,1)} %outw_hbm.1, f32[2,2,512]{2,1,0:T(2,128)} %gain_ref.1, ...), custom_call_target="tpu_custom_call" | custom-call | tf_op jit(solution)/shard_map/swin_pair/pallas_call | solution.py:379
  66.4 1.8 %copy.13 = bf16[12,36,512]{2,1,0:T(8,128)(2,1)} copy(bf16[12,36,512]{2,1,0:T(8,128)(2,1)} %swin_pair.1) | data formatting | bytes 884736
  (1 shorter events, 0.0 us)

commit v3 on v2

--- a/solution.py
+++ b/solution.py
@@ -39,7 +39,7 @@
     tokens_hbm, qkv_hbm, proj_hbm, hid_hbm, outw_hbm,
     gain_ref, mbias_ref, qkvb_ref, hidb_ref, table_ref,
     out_ref,
-    wqkv, wproj, whid, wout, pos_ref, tok_ref, tok32, x32, normed, qkv_ref, heads_ref, hidden_ref, y32,
+    wqkv, wproj, whid, wout, pos_ref, tok_ref, tok32, x32, normed, qkv_ref, heads_ref, hidden_ref, y32, m32,
     stage, rowdiff, coldiff, zrows,
     sa, sb, sc, ra, rb, rc,
     local_sem, psend, precv, xsend, xrecv, ysend, yrecv, fsend, frecv, hsend, hrecv,
@@ -199,7 +199,7 @@
         for rb in rows:
             positions(rb)
 
-    def block(layer, hooks):
+    def block(layer, targets, travel, stay, hooks):
         for w in range(nwin):
             rows = slice(w * AREA, (w + 1) * AREA)
             normed[rows, :] = layer_norm(
@@ -251,40 +251,43 @@
             jnp.dot(heads_ref[...], wproj[layer], preferred_element_type=jnp.float32)
             + mbias_ref[layer, 2:3, :]
         )
-        for w in range(nwin):
-            rows = slice(w * AREA, (w + 1) * AREA)
-            normed[rows, :] = layer_norm(
-                y32[rows, :], gain_ref[layer, 1:2, :], mbias_ref[layer, 1:2, :]
-            ).astype(jnp.bfloat16)
         hooks[2 + nwin]()
+        mlp(layer, [*travel[0], *travel[1], *travel[2]], hooks[3 + nwin])
+        copies, at = [], 0
+        for which, (source, landing) in enumerate(((sa, ra), (sb, rb), (sc, rc))):
+            size = len(travel[which]) * PATCH
+            source[layer] = m32[at : at + size, :].astype(jnp.bfloat16)
+            at += size
+            copy = remote(
+                source.at[layer], landing.at[layer], hsend.at[layer, which], hrecv.at[layer, which], targets[which]
+            )
+            copy.start()
+            copies.append(copy)
+        mlp(layer, stay, nothing)
+        return copies
+
+    def mlp(layer, patches, before_output):
+        rows = slice(0, -(-len(patches) * PATCH // 16) * 16)
+        for at, (half, p) in enumerate(patches):
+            first = base(half, p)
+            m32[at * PATCH : (at + 1) * PATCH, :] = y32[first : first + PATCH, :]
+        normed[rows, :] = layer_norm(
+            m32[rows, :], gain_ref[layer, 1:2, :], mbias_ref[layer, 1:2, :]
+        ).astype(jnp.bfloat16)
         chunk = 512
         for c in range(whid.shape[2] // chunk):
             cols = slice(c * chunk, (c + 1) * chunk)
             pre = (
-                jnp.dot(normed[...], whid[layer, :, cols], preferred_element_type=jnp.float32)
+                jnp.dot(normed[rows, :], whid[layer, :, cols], preferred_element_type=jnp.float32)
                 + hidb_ref[layer : layer + 1, cols]
             )
-            hidden_ref[:, cols] = (0.5 * pre * (1.0 + lax.erf(pre * float(np.sqrt(0.5))))).astype(jnp.bfloat16)
-        hooks[3 + nwin]()
-        final = y32[...] + (
-            jnp.dot(hidden_ref[...], wout[layer], preferred_element_type=jnp.float32)
+            hidden_ref[rows, cols] = (0.5 * pre * (1.0 + lax.erf(pre * float(np.sqrt(0.5))))).astype(jnp.bfloat16)
+        before_output()
+        final = m32[rows, :] + (
+            jnp.dot(hidden_ref[rows, :], wout[layer], preferred_element_type=jnp.float32)
             + mbias_ref[layer, 3:4, :]
         )
-        y32[...] = final.astype(jnp.bfloat16).astype(jnp.float32)
-
-    def exchange(k, targets, patches):
-        copies = []
-        bufs = ((sa, ra), (sb, rb), (sc, rc))
-        for which, (source, landing) in enumerate(bufs):
-            listed = patches[which]
-            for at, (half, p) in enumerate(listed):
-                first = base(half, p)
-                stage[at * PATCH : (at + 1) * PATCH, :] = y32[first : first + PATCH, :]
-            source[k] = stage[0 : len(listed) * PATCH, :].astype(jnp.bfloat16)
-            copy = remote(source.at[k], landing.at[k], hsend.at[k, which], hrecv.at[k, which], targets[which])
-            copy.start()
-            copies.append(copy)
-        return copies
+        m32[rows, :] = final.astype(jnp.bfloat16).astype(jnp.float32)
 
     def nothing():
         pass
@@ -296,7 +299,10 @@
 
         return run
 
-    block(0, [
+    m32[...] = jnp.zeros_like(m32)
+    travel = ([(0, p) for p in range(1, ncols)], [(1, 0)], [(0, 0)])
+    stay = [(1, p) for p in range(1, ncols)]
+    copies = block(0, back, travel, stay, [
         steps(
             (position_range, range(0, 5)), (forward_x, 0), (position_range, range(5, 8)), (forward_x, 1),
             (position_range, range(8, WIN)), (forward_y, 0), (forward_x, 2), (ready, 0),
@@ -308,12 +314,9 @@
         steps((forward_x, 4), (ready, 2)),
         steps((forward_y, 3), (forward_x, 5), (ready, 3)),
     ])
-    copies = exchange(0, back, (
-        [(0, p) for p in range(1, ncols)], [(1, 0)], [(0, 0)],
-    ))
-    for p in range(1, ncols):
-        first, at = base(1, p), base(0, p - 1)
-        x32[at : at + PATCH, :] = y32[first : first + PATCH, :]
+    for p in range(ncols - 1):
+        at = base(0, p)
+        x32[at : at + PATCH, :] = m32[p * PATCH : (p + 1) * PATCH, :]
     steps((forward_y, 4), (forward_x, 6), (forward_y, 5))()
     for copy in copies:
         copy.wait()
@@ -326,7 +329,9 @@
     at = base(1, ncols - 1)
     x32[at : at + PATCH, :] = rc[0].astype(jnp.float32)
 
-    block(1, [
+    travel = ([(1, p) for p in range(ncols - 1)], [(0, ncols - 1)], [(1, ncols - 1)])
+    stay = [(0, p) for p in range(ncols - 1)]
+    copies = block(1, forth, travel, stay, [
         steps((ready, 4), (forward_x, 7)),
         steps((forward_y, 6)),
         nothing,
@@ -335,10 +340,6 @@
         steps((ready, 6)),
         steps((ready, 7)),
     ])
-    copies = exchange(1, forth, (
-        [(1, p) for p in range(ncols - 1)], [(0, ncols - 1)], [(1, ncols - 1)],
-    ))
-
     def put(source, start, half, p):
         for r in range(HALF):
             tok32[half * HALF + r, p * HALF : (p + 1) * HALF, :] = source[
@@ -346,7 +347,7 @@
             ]
 
     for p in range(ncols - 1):
-        put(y32, base(0, p), 1, p + 1)
+        put(m32, p * PATCH, 1, p + 1)
     for copy in copies:
         copy.wait()
     stage[...] = ra[1].astype(jnp.float32)
@@ -392,6 +393,7 @@
             pltpu.VMEM((count, channels), bf16),
             pltpu.VMEM((count, hid_w.shape[2]), bf16),
             pltpu.VMEM((count, channels), f32),
+            pltpu.VMEM((-(-(hop + 2 * PATCH) // 16) * 16, channels), f32),
             pltpu.VMEM((hop, channels), f32),
             pltpu.VMEM((AREA, GROUP * AREA), f32),
             pltpu.VMEM((AREA, GROUP * AREA), f32),

time: 68.4 us -> 67.3 us (0.984)
  Pallas kernels: 63.9 us -> 62.7 us
    pallas_call x1, Pallas kernels: 63.9 us -> 62.7 us  [local(): pl.pallas_call(functools.partial(kernel, sizes), out_shape=jax.ShapeDtype...]
where the time goes in v3:
time: 67.3 us; the launch traced here: 67.1 us
  Pallas kernels  62.7 us (93%)
  local copies, waits for them, and re-layouts  4.25 us (6%)
    pallas_call x1, Pallas kernels, local(): pl.pallas_call(functools.partial(kernel, sizes), out_shape=jax.ShapeDtype...  62.7 us
    unnamed x1, local copies, waits for them, and re-layouts  1.84 us

profile of v3, /device:TPU:0, one launch (start us, length us, event | category | flops | bytes accessed | tf_op | source)
XLA Modules:
  0.0 67.1 jit_solution(2346935165427842293)
XLA Ops:
  0.0 1.1 %reverse.3 = f32[2,16,23,23]{3,1,2,0:T(8,128)S(1)} reverse(f32[2,16,23,23]{3,1,2,0:T(8,128)} %param.19), dimensions={3} | reverse | bytes 135424 | tf_op jit(solution)/shard_map/reverse
  1.2 0.3 copy.11
  1.5 0.1 pad.8
  1.6 0.2 reshape.7
  1.8 0.7 pad.9.table_ref
  2.5 62.7 %swin_pair.1 = bf16[12,36,512]{2,1,0:T(8,128)(2,1)} custom-call(bf16[12,36,512]{2,1,0:T(8,128)(2,1)} %tokens_hbm.1, bf16[2,128,1536]{2,1,0:T(8,128)(2,1)} %qkv_hbm.1, bf16[2,128,512]{2,1,0:T(8,128)(2,1)} %proj_hbm.1, bf16[2,128,2048]{2,1,0:T(8,128)(2,1)} %hid_hbm.1, bf16[2,512,512]{2,1,0:T(8,128)(2,1)} %outw_hbm.1, f32[2,2,512]{2,1,0:T(2,128)} %gain_ref.1, ...), custom_call_target="tpu_custom_call" | custom-call | tf_op jit(solution)/shard_map/swin_pair/pallas_call | solution.py:380
  65.2 1.8 %copy.13 = bf16[12,36,512]{2,1,0:T(8,128)(2,1)} copy(bf16[12,36,512]{2,1,0:T(8,128)(2,1)} %swin_pair.1) | data formatting | bytes 884736
  (1 shorter events, 0.0 us)
